TPU v7x, 32 devices: a whole 2x2x4 slice. The times are simulated.
32 devices in a mesh: slab: 8 (over z, x), blk: 4 (over y, core).
Axes of the slice: x: 2, y: 2, z: 4, core: 2. Of those that a mesh axis runs over, the one named last changes fastest.
Arguments:
- incident: float32 [16, 2, 336, 128], P('slab', None, 'blk'), may hold values from -6 to 6
- mie_coef: float32 [16, 2, 336], P('slab', None, 'blk'), may hold values from -0.6 to 0.6
- translation: bfloat16 [16, 8, 2, 336, 336], P('slab', None, None, 'blk'), may hold values from -0.078125 to 0.078125
- pair_shift: int32 [16, 8], P('slab'), may hold values from -1 to 1
- pair_member: int32 [16, 8], P('slab'), may hold values from 0 to 1
- positions: float32 [16, 3], P('slab'), may hold values from 0 to 1
- wave_index: int32 [256, 3], replicated, may hold values from -4 to 4
- plane_coef: bfloat16 [256, 2, 336], replicated, may hold values from -0.25 to 0.25
- ewald_weight: float32 [256], replicated, may hold values from 0.002 to 0.04
Outputs:
- basis_next: float32 [16, 2, 336, 128], P('slab', None, 'blk')
- residual: float32 [16, 2, 336, 128], P('slab', None, 'blk')
- hessenberg: float32 [9, 128], replicated
Inputs may be any that keep to these rules, and one draw needn't show every extreme that they name: `pair_shift`: each pair's source sphere lies in the target's slab or in one of the two slabs beside it on the periodic cycle of slabs.
All inputs are finite; a program needn't handle non-finite values.
Results may differ from a plain program's by a relative error of at most 0.004.
Values may be sent and summed in bfloat16 or wider, within the bound.
No kernel may reach another device: no remote copies, remote signals or barrier semaphores. Data moves between devices by JAX's collectives and lax.ppermute only.
A program may use at most 64 MiB of HBM per device.

v0:
```python
import jax
import jax.numpy as jnp
from jax import lax
from jax.sharding import PartitionSpec as P

two_pi = 6.283185307179586
epsilon = 1e-06
highest = lax.Precision.HIGHEST


def with_halo(cells, sides, width):
    for axis, dim in sides:
        count = lax.axis_size(axis)
        head = lax.slice_in_dim(cells, 0, width, axis=dim)
        tail = lax.slice_in_dim(cells, cells.shape[dim] - width, cells.shape[dim], axis=dim)
        cells = jnp.concatenate(
            [
                lax.ppermute(tail, axis, [(i, (i + 1) % count) for i in range(count)]),
                cells,
                lax.ppermute(head, axis, [((i + 1) % count, i) for i in range(count)]),
            ],
            axis=dim,
        )
    return cells


def complex_scale(coef_pair, basis):
    part_re = coef_pair[0] * basis[:, 0] - coef_pair[1] * basis[:, 1]
    part_im = coef_pair[0] * basis[:, 1] + coef_pair[1] * basis[:, 0]
    return jnp.stack([part_re, part_im], axis=1)


def inner_sum(left, right):
    part_re = jnp.sum(left[:, 0] * right[:, 0] + left[:, 1] * right[:, 1], axis=(0, 1))
    part_im = jnp.sum(left[:, 0] * right[:, 1] - left[:, 1] * right[:, 0], axis=(0, 1))
    return jnp.stack([part_re, part_im])


def plane_sums(projected, cos_part, sin_part):
    part_re = projected[:, 0, :, 0] - projected[:, 1, :, 1]
    part_im = projected[:, 0, :, 1] + projected[:, 1, :, 0]
    sum_re = jnp.sum(cos_part[:, :, None] * part_re + sin_part[:, :, None] * part_im, axis=1)
    sum_im = jnp.sum(cos_part[:, :, None] * part_im - sin_part[:, :, None] * part_re, axis=1)
    return jnp.stack([sum_re, sum_im], axis=1)


def plane_field(totals, coef_full, cos_part, sin_part, weights):
    total_re = totals[:, 0][:, None, :]
    total_im = totals[:, 1][:, None, :]
    turn_re = weights[:, None, None] * (
        cos_part[:, :, None] * total_re - sin_part[:, :, None] * total_im
    )
    turn_im = weights[:, None, None] * (
        cos_part[:, :, None] * total_im + sin_part[:, :, None] * total_re
    )
    turned = jnp.stack([turn_re, turn_im], axis=1)
    projected = jnp.einsum("gac,gbjn->jabcn", coef_full, turned, precision=highest)
    return jnp.stack(
        [projected[:, 0, 0] + projected[:, 1, 1], projected[:, 0, 1] - projected[:, 1, 0]], axis=1
    )


def apply_operator(
    vector, mie_coef, translation, source_rows, cos_part, sin_part, plane_coef, ewald_weight
):
    sphere_count = vector.shape[0]
    row_count = vector.shape[2]
    wave_count = plane_coef.shape[0]
    rounded = vector.astype(jnp.bfloat16)
    full_field = lax.all_gather(rounded, "blk", axis=2, tiled=True)
    extended = with_halo(full_field, (("slab", 0),), sphere_count)
    pair_count = translation.shape[0] * translation.shape[1]
    flat_trans = translation.reshape(pair_count, 2, row_count, translation.shape[4])
    sources = jnp.take(extended, source_rows, axis=0)
    product = jnp.einsum(
        "parc,pzcn->pazrn", flat_trans, sources, preferred_element_type=jnp.float32
    )
    near_re = product[:, 0, 0] - product[:, 1, 1]
    near_im = product[:, 0, 1] + product[:, 1, 0]
    near = (
        jnp.stack([near_re, near_im], axis=1)
        .reshape(sphere_count, translation.shape[1], 2, row_count, vector.shape[3])
        .sum(axis=1)
    )
    row_start = lax.axis_index("blk") * row_count
    coef_rows = lax.dynamic_slice_in_dim(plane_coef, row_start, row_count, 2)
    slice_count = wave_count // lax.axis_size("blk")
    wave_start = lax.axis_index("blk") * slice_count
    coef_slice = lax.dynamic_slice_in_dim(plane_coef, wave_start, slice_count, 0)
    cos_slice = lax.dynamic_slice_in_dim(cos_part, wave_start, slice_count, 0)
    sin_slice = lax.dynamic_slice_in_dim(sin_part, wave_start, slice_count, 0)
    projected = jnp.einsum(
        "gac,jbcn->gajbn", coef_slice, full_field, preferred_element_type=jnp.float32
    )
    partial_sums = plane_sums(projected, cos_slice, sin_slice)
    slice_total = lax.psum(partial_sums, "slab")
    totals = lax.all_gather(slice_total, "blk", axis=0, tiled=True)
    far = plane_field(totals, coef_rows.astype(jnp.float32), cos_part, sin_part, ewald_weight)
    summed = near + far
    scaled_re = (
        mie_coef[:, 0][:, :, None] * summed[:, 0] - mie_coef[:, 1][:, :, None] * summed[:, 1]
    )
    scaled_im = (
        mie_coef[:, 0][:, :, None] * summed[:, 1] + mie_coef[:, 1][:, :, None] * summed[:, 0]
    )
    return vector - jnp.stack([scaled_re, scaled_im], axis=1)


def squared(field):
    return jnp.sum(field * field, axis=(0, 1, 2))


def per_device(
    incident,
    mie_coef,
    translation,
    pair_shift,
    pair_member,
    positions,
    wave_index,
    plane_coef,
    ewald_weight,
):
    sphere_count = incident.shape[0]
    entries = sphere_count * lax.axis_size("slab") * incident.shape[2] * lax.axis_size("blk")
    source_rows = ((pair_shift + 1) * sphere_count + pair_member).reshape(-1)
    angles = two_pi * jnp.sum(
        wave_index.astype(jnp.float32)[:, None, :] * positions[None, :, :], axis=-1
    )
    cos_part = jnp.cos(angles)
    sin_part = jnp.sin(angles)

    def operator(vector):
        return apply_operator(
            vector, mie_coef, translation, source_rows, cos_part, sin_part, plane_coef, ewald_weight
        )

    start_total = lax.psum(squared(incident), ("slab", "blk"))
    beta = jnp.sqrt(start_total / entries + epsilon)
    first = incident / beta
    image = operator(first)
    proj_sum = lax.psum(inner_sum(first, image), ("slab", "blk"))
    h_one_one = proj_sum / entries
    image = image - complex_scale(h_one_one, first)
    first_total = lax.psum(squared(image), ("slab", "blk"))
    h_two_one = jnp.sqrt(first_total / entries + epsilon)
    basis_next = image / h_two_one
    image = operator(basis_next)
    h_one_two = lax.psum(inner_sum(first, image), ("slab", "blk")) / entries
    image = image - complex_scale(h_one_two, first)
    h_two_two = lax.psum(inner_sum(basis_next, image), ("slab", "blk")) / entries
    residual = image - complex_scale(h_two_two, basis_next)
    last_total = lax.psum(squared(residual), ("slab", "blk"))
    h_three_two = jnp.sqrt(last_total / entries + epsilon)
    hessenberg = jnp.stack(
        [
            beta,
            h_one_one[0],
            h_one_one[1],
            h_two_one,
            h_one_two[0],
            h_one_two[1],
            h_two_two[0],
            h_two_two[1],
            h_three_two,
        ]
    )
    return (basis_next, residual, hessenberg)


def solution(mesh):
    placed = (
        P("slab", None, "blk", None),
        P("slab", None, "blk"),
        P("slab", None, None, "blk", None),
        P("slab", None),
        P("slab", None),
        P("slab", None),
        P(),
        P(),
        P(),
    )
    return jax.shard_map(
        per_device,
        mesh=mesh,
        in_specs=placed,
        out_specs=(P("slab", None, "blk", None), P("slab", None, "blk", None), P()),
        check_vma=False,
    )
```

profile of v0, /device:TPU:0, one launch (start us, length us, event | category | flops | bytes accessed | tf_op | source)
XLA Modules:
  0.0 478.9 jit_solution(5836638708583548738)
XLA Ops:
  8.5 42.0 %psum.56 = f32[128]{0:T(128)S(1)} all-reduce(f32[128]{0:T(128)S(1)} %multiply_reduce_fusion.2), channel_id=1, replica_groups=mesh['slab'=8,'blk'=4] {'slab','blk'}, use_global_device_ids=true, to_apply=%region_1.0 | all-reduce | flops 128 | bytes 1024 | tf_op jit(solution)/shard_map/psum | solution.py:138
  52.0 7.0 %all_gather.12 = bf16[2,2,336,128]{3,1,0,2:T(2,128)(2,1)S(1)} all-gather(bf16[2,2,84,128]{3,1,0,2:T(2,128)(2,1)S(1)} %copy.52), channel_id=1, replica_groups=mesh['slab'=8,'blk'=4] {'blk'}, dimensions={2}, use_global_device_ids=true | all-gather | bytes 430080 | tf_op jit(solution)/shard_map/all_gather | solution.py:70
  59.0 1.3 collective-permute-start
  60.3 3.4 collective-permute-start.1
  65.3 1.3 fusion.24
  69.1 65.3 %all-reduce.3.cloned.1.call-done = f32[64,2,128]{2,0,1:T(8,128)} async-done(((f32[64,2,128]{2,0,1:T(8,128)}), f32[64,2,128]{2,0,1:T(8,128)}) %all-reduce.3.cloned.1.call-update) | async-done | bytes 65552 | tf_op jit(solution)/shard_map/psum | solution.py:96
  134.3 6.0 %all_gather.13 = f32[256,2,128]{2,0,1:T(8,128)S(1)} all-gather(f32[64,2,128]{2,0,1:T(8,128)} %all-reduce.3.cloned.1.call-done), channel_id=1, replica_groups=mesh['slab'=8,'blk'=4] {'blk'}, dimensions={0}, use_global_device_ids=true | all-gather | bytes 327680 | tf_op jit(solution)/shard_map/all_gather | solution.py:97
  140.6 1.3 convolution_bitcast_fusion.1
  142.7 2.5 pad_maximum_fusion
  145.2 8.9 %gather_fusion = bf16[16,2,336,128]{3,1,2,0:T(2,128)(2,1)} fusion(bf16[6,2,336,128]{3,1,0,2:T(2,128)(2,1)S(1)} %pad_maximum_fusion, s32[1024]{0:T(1024)S(1)} %pad_clamp_fusion), kind=kCustom, calls=%fused_computation.clone | custom fusion | bytes 5505088 | tf_op jit(solution)/shard_map/jit(_take)/gather | solution.py:74
  154.1 4.2 fusion.4
  160.3 40.4 %psum.58 = f32[2,128]{1,0:T(2,128)S(1)} all-reduce(f32[2,128]{1,0:T(2,128)S(1)} %pad_maximum_fusion.4), channel_id=1, replica_groups=mesh['slab'=8,'blk'=4] {'slab','blk'}, use_global_device_ids=true, to_apply=%region_9.11 | all-reduce | flops 256 | bytes 2048 | tf_op jit(solution)/shard_map/psum | solution.py:142
  200.8 39.0 %psum.59 = f32[128]{0:T(128)S(1)} all-reduce(f32[128]{0:T(128)S(1)} %multiply_reduce_fusion.1), channel_id=1, replica_groups=mesh['slab'=8,'blk'=4] {'slab','blk'}, use_global_device_ids=true, to_apply=%region_11.13 | all-reduce | flops 128 | bytes 1024 | tf_op jit(solution)/shard_map/psum | solution.py:145
  240.5 7.0 %all_gather.14 = bf16[2,2,336,128]{3,1,0,2:T(2,128)(2,1)S(1)} all-gather(bf16[2,2,84,128]{3,1,0,2:T(2,128)(2,1)S(1)} %copy.62), channel_id=1, replica_groups=mesh['slab'=8,'blk'=4] {'blk'}, dimensions={2}, use_global_device_ids=true | all-gather | bytes 430080 | tf_op jit(solution)/shard_map/all_gather | solution.py:70
  248.5 1.4 collective-permute-start.2
  249.9 3.4 collective-permute-start.3
  254.1 70.2 %all-reduce.5.cloned.1.call-done = f32[64,2,128]{2,0,1:T(8,128)} async-done(((f32[64,2,128]{2,0,1:T(8,128)}), f32[64,2,128]{2,0,1:T(8,128)}) %all-reduce.5.cloned.1.call-update) | async-done | bytes 65552 | tf_op jit(solution)/shard_map/psum | solution.py:96
  324.3 6.0 %all_gather.15 = f32[256,2,128]{2,0,1:T(8,128)S(1)} all-gather(f32[64,2,128]{2,0,1:T(8,128)} %all-reduce.5.cloned.1.call-done), channel_id=1, replica_groups=mesh['slab'=8,'blk'=4] {'blk'}, dimensions={0}, use_global_device_ids=true | all-gather | bytes 327680 | tf_op jit(solution)/shard_map/all_gather | solution.py:97
  331.6 2.6 pad_maximum_fusion.1
  334.2 9.0 %gather_fusion.1 = bf16[16,2,336,128]{3,1,2,0:T(2,128)(2,1)} fusion(bf16[6,2,336,128]{3,1,0,2:T(2,128)(2,1)S(1)} %pad_maximum_fusion.1, s32[1024]{0:T(1024)} %copy-done.9), kind=kCustom, calls=%fused_computation.1.clone | custom fusion | bytes 5505088 | tf_op jit(solution)/shard_map/jit(_take)/gather | solution.py:74
  343.1 4.2 fusion.5
  349.4 40.4 %psum.61 = f32[2,128]{1,0:T(2,128)S(1)} all-reduce(f32[2,128]{1,0:T(2,128)S(1)} %pad_maximum_fusion.5), channel_id=1, replica_groups=mesh['slab'=8,'blk'=4] {'slab','blk'}, use_global_device_ids=true, to_apply=%region_18.20 | all-reduce | flops 256 | bytes 2048 | tf_op jit(solution)/shard_map/psum | solution.py:149
  390.0 39.1 %psum.62 = f32[2,128]{1,0:T(2,128)S(1)} all-reduce(f32[2,128]{1,0:T(2,128)S(1)} %pad_maximum_fusion.6), channel_id=1, replica_groups=mesh['slab'=8,'blk'=4] {'slab','blk'}, use_global_device_ids=true, to_apply=%region_21.23 | all-reduce | flops 256 | bytes 2048 | tf_op jit(solution)/shard_map/psum | solution.py:151
  429.2 40.9 %psum.63 = f32[128]{0:T(128)S(1)} all-reduce(f32[128]{0:T(128)S(1)} %get-tuple-element.23), channel_id=1, replica_groups=mesh['slab'=8,'blk'=4] {'slab','blk'}, use_global_device_ids=true, to_apply=%region_23.25 | all-reduce | flops 128 | bytes 1024 | tf_op jit(solution)/shard_map/psum | solution.py:153
  (101 shorter events, 18.0 us)
Async XLA Ops:
  7.2 151.1 %copy-start = (bf16[2,8,2,84,336]{4,2,3,1,0:T(2,128)(2,1)S(1)}, bf16[2,8,2,84,336]{4,2,3,1,0:T(2,128)(2,1)}, u32[]{:S(2)}) copy-start(bf16[2,8,2,84,336]{4,2,3,1,0:T(2,128)(2,1)} %param.13) | copy-start | bytes 5419012
  7.2 133.1 %copy-start.10 = (f32[256]{0:T(256)S(1)}, f32[256]{0:T(256)}, u32[]{:S(2)}) copy-start(f32[256]{0:T(256)} %param.19) | copy-start | bytes 3076
  7.2 127.1 %all-reduce.3.cloned.1.call-start = ((), (), s32[]{:S(2)}) async-start(), calls=%async_computation | async-start | bytes 131072 | tf_op jit(solution)/shard_map/psum | solution.py:96
  59.0 82.9 %copy-start.2 = (bf16[2,2,336,128]{3,1,0,2:T(2,128)(2,1)}, bf16[2,2,336,128]{3,1,0,2:T(2,128)(2,1)S(1)}, u32[]{:S(2)}) copy-start(bf16[2,2,336,128]{3,1,0,2:T(2,128)(2,1)S(1)} %all_gather.12) | copy-start | bytes 1032196
  59.0 82.9 %collective-permute-start = (bf16[2,2,336,128]{3,1,0,2:T(2,128)(2,1)S(1)}, bf16[2,2,336,128]{3,1,0,2:T(2,128)(2,1)S(1)}, u32[]{:S(2)}, u32[]{:S(2)}) collective-permute-start(bf16[2,2,336,128]{3,1,0,2:T(2,128)(2,1)S(1)} %all_gather.12), channel_id=1, source_target_pairs={{0,4},{4,8},{8,12},{12,16},{16,20},{20,24},{24,28},{28,0},{1,5},{5... | collective-permute-start | bytes 1032200 | tf_op jit(solution)/shard_map/ppermute | solution.py:18
  60.3 82.4 %collective-permute-start.1 = (bf16[2,2,336,128]{3,1,0,2:T(2,128)(2,1)S(1)}, bf16[2,2,336,128]{3,1,0,2:T(2,128)(2,1)}, u32[]{:S(2)}, u32[]{:S(2)}) collective-permute-start(bf16[2,2,336,128]{3,1,0,2:T(2,128)(2,1)S(1)} %all_gather.12), channel_id=1, source_target_pairs={{4,0},{8,4},{12,8},{16,12},{20,16},{24,20},{28,24},{0,28},{5,1},{9... | collective-permute-start | bytes 1032200 | tf_op jit(solution)/shard_map/ppermute | solution.py:20
  67.4 256.9 %all-reduce.5.cloned.1.call-start = ((), (), s32[]{:S(2)}) async-start(), calls=%async_computation.1 | async-start | bytes 131072 | tf_op jit(solution)/shard_map/psum | solution.py:96
  68.3 85.8 %copy-start.11 = (pred[16]{0:T(512)(128)(4,1)}, pred[16]{0:T(512)(128)(4,1)S(1)}, u32[]{:S(2)}) copy-start(pred[16]{0:T(512)(128)(4,1)S(1)} %compare_and_fusion) | copy-start | bytes 52
  69.1 85.0 %copy-start.9 = (s32[1024]{0:T(1024)}, s32[1024]{0:T(1024)S(1)}, u32[]{:S(2)}) copy-start(s32[1024]{0:T(1024)S(1)} %pad_clamp_fusion) | copy-start | bytes 12292
  141.9 0.7 copy-start.6
  159.2 0.9 copy-start.1
  159.4 88.0 %copy-start.4 = (bf16[256,2,336]{0,2,1:T(8,128)(2,1)S(1)}, bf16[256,2,336]{0,2,1:T(8,128)(2,1)}, u32[]{:S(2)}) copy-start(bf16[256,2,336]{0,2,1:T(8,128)(2,1)} %param.18) | copy-start | bytes 1032196
  200.6 129.9 %copy-start.7 = (f32[2,128]{1,0:T(2,128)}, f32[2,128]{1,0:T(2,128)S(1)}, u32[]{:S(2)}) copy-start(f32[2,128]{1,0:T(2,128)S(1)} %broadcast_multiply_fusion.2) | copy-start | bytes 3076
  247.4 84.2 %copy-start.3 = (bf16[2,2,336,128]{3,1,0,2:T(2,128)(2,1)}, bf16[2,2,336,128]{3,1,0,2:T(2,128)(2,1)S(1)}, u32[]{:S(2)}) copy-start(bf16[2,2,336,128]{3,1,0,2:T(2,128)(2,1)S(1)} %all_gather.14) | copy-start | bytes 1032196
  248.5 83.1 %collective-permute-start.2 = (bf16[2,2,336,128]{3,1,0,2:T(2,128)(2,1)S(1)}, bf16[2,2,336,128]{3,1,0,2:T(2,128)(2,1)}, u32[]{:S(2)}, u32[]{:S(2)}) collective-permute-start(bf16[2,2,336,128]{3,1,0,2:T(2,128)(2,1)S(1)} %all_gather.14), channel_id=1, source_target_pairs={{0,4},{4,8},{8,12},{12,16},{16,20},{20,24},{24,28},{28,0},{1,5},{5... | collective-permute-start | bytes 1032200 | tf_op jit(solution)/shard_map/ppermute | solution.py:18
  249.9 81.7 %collective-permute-start.3 = (bf16[2,2,336,128]{3,1,0,2:T(2,128)(2,1)S(1)}, bf16[2,2,336,128]{3,1,0,2:T(2,128)(2,1)}, u32[]{:S(2)}, u32[]{:S(2)}) collective-permute-start(bf16[2,2,336,128]{3,1,0,2:T(2,128)(2,1)S(1)} %all_gather.14), channel_id=1, source_target_pairs={{4,0},{8,4},{12,8},{16,12},{20,16},{24,20},{28,24},{0,28},{5,1},{9... | collective-permute-start | bytes 1032200 | tf_op jit(solution)/shard_map/ppermute | solution.py:20
  348.3 0.9 copy-start.5
  348.5 122.2 %copy-start.8 = (f32[2,128]{1,0:T(2,128)S(1)}, f32[2,128]{1,0:T(2,128)}, u32[]{:S(2)}) copy-start(f32[2,128]{1,0:T(2,128)} %copy-done.7) | copy-start | bytes 3076
  348.6 122.2 %copy-start.12 = (f32[1,128]{1,0:T(1,128)S(1)}, f32[1,128]{1,0:T(1,128)}, u32[]{:S(2)}) copy-start(f32[1,128]{1,0:T(1,128)} %get-tuple-element.65) | copy-start | bytes 1540
  348.6 122.2 %copy-start.13 = (f32[1,128]{1,0:T(1,128)S(1)}, f32[1,128]{1,0:T(1,128)}, u32[]{:S(2)}) copy-start(f32[1,128]{1,0:T(1,128)} %get-tuple-element.63) | copy-start | bytes 1540
Sparse Core Ops, SparseCore 0:
  67.5 66.7 all-reduce.2
  248.7 75.5 all-reduce.4
where the time goes:
time: 480 us; the launch traced here: 479 us
  blocking collectives  268 us (56%)
  waiting for transfers between devices  136 us (28%)
  local copies, waits for them, and re-layouts  24.4 us (5%)
  other arithmetic  22.3 us (5%)
  between operations  14.4 us (3%)
  starting transfers between devices  9.58 us (2%)
  matrix products  5.11 us (1%)
    psum x2, waiting for transfers between devices, apply_operator(): slice_total = lax.psum(partial_sums, 'slab')  135 us
    psum x1, blocking collectives, per_device(): start_total = lax.psum(squared(incident), ('slab', 'blk'))  42 us
    psum x1, blocking collectives, per_device(): last_total = lax.psum(squared(residual), ('slab', 'blk'))  40.9 us
    psum x1, blocking collectives, per_device(): h_one_two = lax.psum(inner_sum(first, image), ('slab', 'blk')) / entries  40.4 us
    psum x1, blocking collectives, per_device(): proj_sum = lax.psum(inner_sum(first, image), ('slab', 'blk'))  40.4 us
    psum x1, blocking collectives, per_device(): lax.psum(inner_sum(basis_next, image), ('slab', 'blk')) / entries  39.1 us
    psum x1, blocking collectives, per_device(): first_total = lax.psum(squared(image), ('slab', 'blk'))  39 us
    gather x2, local copies, waits for them, and re-layouts, apply_operator(): sources = jnp.take(extended, source_rows, axis=0)  17.8 us
  transfers between devices with their start and end apart: 6, of which 2 were waited for; matrix products, arithmetic and copies ran while one was open for 2% of the time, Pallas kernels for 0%

commit v1 on v0

--- a/solution.py
+++ b/solution.py
@@ -150,7 +150,7 @@
     image = image - complex_scale(h_one_two, first)
     h_two_two = lax.psum(inner_sum(basis_next, image), ("slab", "blk")) / entries
     residual = image - complex_scale(h_two_two, basis_next)
-    last_total = lax.psum(squared(residual), ("slab", "blk"))
+    last_total = lax.psum(lax.psum(squared(residual), "blk"), "slab")
     h_three_two = jnp.sqrt(last_total / entries + epsilon)
     hessenberg = jnp.stack(
         [

time: 480 us -> 466 us (0.971)
  blocking collectives: 268 us -> 253 us
    psum x1 -> x2, blocking collectives: 40.9 us -> 26.7 us  [per_device(): last_total = lax.psum(lax.psum(squared(residual), 'blk'), 'slab')]
where the time goes in v1:
time: 466 us; the launch traced here: 465 us
  blocking collectives  253 us (54%)
  waiting for transfers between devices  136 us (29%)
  local copies, waits for them, and re-layouts  24.4 us (5%)
  other arithmetic  22.3 us (5%)
  between operations  14.4 us (3%)
  starting transfers between devices  9.58 us (2%)
  matrix products  5.11 us (1%)
    psum x2, waiting for transfers between devices, apply_operator(): slice_total = lax.psum(partial_sums, 'slab')  135 us
    psum x1, blocking collectives, per_device(): start_total = lax.psum(squared(incident), ('slab', 'blk'))  42 us
    psum x1, blocking collectives, per_device(): proj_sum = lax.psum(inner_sum(first, image), ('slab', 'blk'))  40.4 us
    psum x1, blocking collectives, per_device(): h_one_two = lax.psum(inner_sum(first, image), ('slab', 'blk')) / entries  40.2 us
    psum x1, blocking collectives, per_device(): lax.psum(inner_sum(basis_next, image), ('slab', 'blk')) / entries  39.1 us
    psum x1, blocking collectives, per_device(): first_total = lax.psum(squared(image), ('slab', 'blk'))  39 us
    psum x2, blocking collectives, per_device(): last_total = lax.psum(lax.psum(squared(residual), 'blk'), 'slab')  26.7 us
    gather x2, local copies, waits for them, and re-layouts, apply_operator(): sources = jnp.take(extended, source_rows, axis=0)  17.8 us
  transfers between devices with their start and end apart: 6, of which 2 were waited for; matrix products, arithmetic and copies ran while one was open for 2% of the time, Pallas kernels for 0%

profile of v1, /device:TPU:0, one launch (start us, length us, event | category | flops | bytes accessed | tf_op | source)
XLA Modules:
  0.0 464.5 jit_solution(5032423188420116818)
XLA Ops:
  8.5 42.0 %psum.63 = f32[128]{0:T(128)S(1)} all-reduce(f32[128]{0:T(128)S(1)} %multiply_reduce_fusion.2), channel_id=1, replica_groups=mesh['slab'=8,'blk'=4] {'slab','blk'}, use_global_device_ids=true, to_apply=%region_1.0 | all-reduce | flops 128 | bytes 1024 | tf_op jit(solution)/shard_map/psum | solution.py:138
  52.0 7.0 %all_gather.12 = bf16[2,2,336,128]{3,1,0,2:T(2,128)(2,1)S(1)} all-gather(bf16[2,2,84,128]{3,1,0,2:T(2,128)(2,1)S(1)} %copy.52), channel_id=1, replica_groups=mesh['slab'=8,'blk'=4] {'blk'}, dimensions={2}, use_global_device_ids=true | all-gather | bytes 430080 | tf_op jit(solution)/shard_map/all_gather | solution.py:70
  59.0 1.3 collective-permute-start
  60.3 3.4 collective-permute-start.1
  69.1 65.3 %all-reduce.3.cloned.1.call-done = f32[64,2,128]{2,0,1:T(8,128)} async-done(((f32[64,2,128]{2,0,1:T(8,128)}), f32[64,2,128]{2,0,1:T(8,128)}) %all-reduce.3.cloned.1.call-update) | async-done | bytes 65552 | tf_op jit(solution)/shard_map/psum | solution.py:96
  134.3 6.0 %all_gather.13 = f32[256,2,128]{2,0,1:T(8,128)S(1)} all-gather(f32[64,2,128]{2,0,1:T(8,128)} %all-reduce.3.cloned.1.call-done), channel_id=1, replica_groups=mesh['slab'=8,'blk'=4] {'blk'}, dimensions={0}, use_global_device_ids=true | all-gather | bytes 327680 | tf_op jit(solution)/shard_map/all_gather | solution.py:97
  140.6 1.3 convolution_bitcast_fusion.1
  142.7 2.5 pad_maximum_fusion
  145.2 8.9 %gather_fusion = bf16[16,2,336,128]{3,1,2,0:T(2,128)(2,1)} fusion(bf16[6,2,336,128]{3,1,0,2:T(2,128)(2,1)S(1)} %pad_maximum_fusion, s32[1024]{0:T(1024)S(1)} %pad_clamp_fusion), kind=kCustom, calls=%fused_computation.clone | custom fusion | bytes 5505088 | tf_op jit(solution)/shard_map/jit(_take)/gather | solution.py:74
  154.1 4.2 fusion.4
  160.3 40.4 %psum.65 = f32[2,128]{1,0:T(2,128)S(1)} all-reduce(f32[2,128]{1,0:T(2,128)S(1)} %pad_maximum_fusion.4), channel_id=1, replica_groups=mesh['slab'=8,'blk'=4] {'slab','blk'}, use_global_device_ids=true, to_apply=%region_9.11 | all-reduce | flops 256 | bytes 2048 | tf_op jit(solution)/shard_map/psum | solution.py:142
  200.8 39.0 %psum.66 = f32[128]{0:T(128)S(1)} all-reduce(f32[128]{0:T(128)S(1)} %multiply_reduce_fusion.1), channel_id=1, replica_groups=mesh['slab'=8,'blk'=4] {'slab','blk'}, use_global_device_ids=true, to_apply=%region_11.13 | all-reduce | flops 128 | bytes 1024 | tf_op jit(solution)/shard_map/psum | solution.py:145
  240.5 7.0 %all_gather.14 = bf16[2,2,336,128]{3,1,0,2:T(2,128)(2,1)S(1)} all-gather(bf16[2,2,84,128]{3,1,0,2:T(2,128)(2,1)S(1)} %copy.62), channel_id=1, replica_groups=mesh['slab'=8,'blk'=4] {'blk'}, dimensions={2}, use_global_device_ids=true | all-gather | bytes 430080 | tf_op jit(solution)/shard_map/all_gather | solution.py:70
  248.5 1.4 collective-permute-start.2
  249.9 3.4 collective-permute-start.3
  254.1 70.2 %all-reduce.5.cloned.1.call-done = f32[64,2,128]{2,0,1:T(8,128)} async-done(((f32[64,2,128]{2,0,1:T(8,128)}), f32[64,2,128]{2,0,1:T(8,128)}) %all-reduce.5.cloned.1.call-update) | async-done | bytes 65552 | tf_op jit(solution)/shard_map/psum | solution.py:96
  324.3 6.0 %all_gather.15 = f32[256,2,128]{2,0,1:T(8,128)S(1)} all-gather(f32[64,2,128]{2,0,1:T(8,128)} %all-reduce.5.cloned.1.call-done), channel_id=1, replica_groups=mesh['slab'=8,'blk'=4] {'blk'}, dimensions={0}, use_global_device_ids=true | all-gather | bytes 327680 | tf_op jit(solution)/shard_map/all_gather | solution.py:97
  331.6 2.6 pad_maximum_fusion.1
  334.2 9.0 %gather_fusion.1 = bf16[16,2,336,128]{3,1,2,0:T(2,128)(2,1)} fusion(bf16[6,2,336,128]{3,1,0,2:T(2,128)(2,1)S(1)} %pad_maximum_fusion.1, s32[1024]{0:T(1024)} %copy-done.9), kind=kCustom, calls=%fused_computation.1.clone | custom fusion | bytes 5505088 | tf_op jit(solution)/shard_map/jit(_take)/gather | solution.py:74
  343.1 4.2 fusion.5
  349.4 40.2 %psum.68 = f32[2,128]{1,0:T(2,128)S(1)} all-reduce(f32[2,128]{1,0:T(2,128)S(1)} %pad_maximum_fusion.5), channel_id=1, replica_groups=mesh['slab'=8,'blk'=4] {'slab','blk'}, use_global_device_ids=true, to_apply=%region_18.20 | all-reduce | flops 256 | bytes 2048 | tf_op jit(solution)/shard_map/psum | solution.py:149
  389.8 39.1 %psum.69 = f32[2,128]{1,0:T(2,128)S(1)} all-reduce(f32[2,128]{1,0:T(2,128)S(1)} %pad_maximum_fusion.6), channel_id=1, replica_groups=mesh['slab'=8,'blk'=4] {'slab','blk'}, use_global_device_ids=true, to_apply=%region_21.23 | all-reduce | flops 256 | bytes 2048 | tf_op jit(solution)/shard_map/psum | solution.py:151
  428.9 6.3 %psum.70 = f32[128]{0:T(128)S(1)} all-reduce(f32[128]{0:T(128)S(1)} %get-tuple-element.23), channel_id=1, replica_groups=mesh['slab'=8,'blk'=4] {'blk'}, use_global_device_ids=true, to_apply=%region_23.25 | all-reduce | flops 128 | bytes 1024 | tf_op jit(solution)/shard_map/psum | solution.py:153
  435.2 20.4 %psum.71 = f32[128]{0:T(128)S(1)} all-reduce(f32[128]{0:T(128)S(1)} %psum.70), channel_id=1, replica_groups=mesh['slab'=8,'blk'=4] {'slab'}, use_global_device_ids=true, to_apply=%region_24.26 | all-reduce | flops 128 | bytes 1024 | tf_op jit(solution)/shard_map/psum | solution.py:153
  (102 shorter events, 19.2 us)
Async XLA Ops:
  7.2 151.1 %copy-start = (bf16[2,8,2,84,336]{4,2,3,1,0:T(2,128)(2,1)S(1)}, bf16[2,8,2,84,336]{4,2,3,1,0:T(2,128)(2,1)}, u32[]{:S(2)}) copy-start(bf16[2,8,2,84,336]{4,2,3,1,0:T(2,128)(2,1)} %param.13) | copy-start | bytes 5419012
  7.2 133.1 %copy-start.10 = (f32[256]{0:T(256)S(1)}, f32[256]{0:T(256)}, u32[]{:S(2)}) copy-start(f32[256]{0:T(256)} %param.19) | copy-start | bytes 3076
  7.2 127.1 %all-reduce.3.cloned.1.call-start = ((), (), s32[]{:S(2)}) async-start(), calls=%async_computation | async-start | bytes 131072 | tf_op jit(solution)/shard_map/psum | solution.py:96
  59.0 82.9 %copy-start.2 = (bf16[2,2,336,128]{3,1,0,2:T(2,128)(2,1)}, bf16[2,2,336,128]{3,1,0,2:T(2,128)(2,1)S(1)}, u32[]{:S(2)}) copy-start(bf16[2,2,336,128]{3,1,0,2:T(2,128)(2,1)S(1)} %all_gather.12) | copy-start | bytes 1032196
  59.0 82.9 %collective-permute-start = (bf16[2,2,336,128]{3,1,0,2:T(2,128)(2,1)S(1)}, bf16[2,2,336,128]{3,1,0,2:T(2,128)(2,1)S(1)}, u32[]{:S(2)}, u32[]{:S(2)}) collective-permute-start(bf16[2,2,336,128]{3,1,0,2:T(2,128)(2,1)S(1)} %all_gather.12), channel_id=1, source_target_pairs={{0,4},{4,8},{8,12},{12,16},{16,20},{20,24},{24,28},{28,0},{1,5},{5... | collective-permute-start | bytes 1032200 | tf_op jit(solution)/shard_map/ppermute | solution.py:18
  60.3 82.4 %collective-permute-start.1 = (bf16[2,2,336,128]{3,1,0,2:T(2,128)(2,1)S(1)}, bf16[2,2,336,128]{3,1,0,2:T(2,128)(2,1)}, u32[]{:S(2)}, u32[]{:S(2)}) collective-permute-start(bf16[2,2,336,128]{3,1,0,2:T(2,128)(2,1)S(1)} %all_gather.12), channel_id=1, source_target_pairs={{4,0},{8,4},{12,8},{16,12},{20,16},{24,20},{28,24},{0,28},{5,1},{9... | collective-permute-start | bytes 1032200 | tf_op jit(solution)/shard_map/ppermute | solution.py:20
  67.4 256.9 %all-reduce.5.cloned.1.call-start = ((), (), s32[]{:S(2)}) async-start(), calls=%async_computation.1 | async-start | bytes 131072 | tf_op jit(solution)/shard_map/psum | solution.py:96
  68.3 85.8 %copy-start.11 = (pred[16]{0:T(512)(128)(4,1)}, pred[16]{0:T(512)(128)(4,1)S(1)}, u32[]{:S(2)}) copy-start(pred[16]{0:T(512)(128)(4,1)S(1)} %compare_and_fusion) | copy-start | bytes 52
  69.1 85.0 %copy-start.9 = (s32[1024]{0:T(1024)}, s32[1024]{0:T(1024)S(1)}, u32[]{:S(2)}) copy-start(s32[1024]{0:T(1024)S(1)} %pad_clamp_fusion) | copy-start | bytes 12292
  141.9 0.7 copy-start.6
  159.2 0.9 copy-start.1
  159.4 88.0 %copy-start.4 = (bf16[256,2,336]{0,2,1:T(8,128)(2,1)S(1)}, bf16[256,2,336]{0,2,1:T(8,128)(2,1)}, u32[]{:S(2)}) copy-start(bf16[256,2,336]{0,2,1:T(8,128)(2,1)} %param.18) | copy-start | bytes 1032196
  200.6 129.9 %copy-start.7 = (f32[2,128]{1,0:T(2,128)}, f32[2,128]{1,0:T(2,128)S(1)}, u32[]{:S(2)}) copy-start(f32[2,128]{1,0:T(2,128)S(1)} %broadcast_multiply_fusion.2) | copy-start | bytes 3076
  247.4 84.2 %copy-start.3 = (bf16[2,2,336,128]{3,1,0,2:T(2,128)(2,1)}, bf16[2,2,336,128]{3,1,0,2:T(2,128)(2,1)S(1)}, u32[]{:S(2)}) copy-start(bf16[2,2,336,128]{3,1,0,2:T(2,128)(2,1)S(1)} %all_gather.14) | copy-start | bytes 1032196
  248.5 83.1 %collective-permute-start.2 = (bf16[2,2,336,128]{3,1,0,2:T(2,128)(2,1)S(1)}, bf16[2,2,336,128]{3,1,0,2:T(2,128)(2,1)}, u32[]{:S(2)}, u32[]{:S(2)}) collective-permute-start(bf16[2,2,336,128]{3,1,0,2:T(2,128)(2,1)S(1)} %all_gather.14), channel_id=1, source_target_pairs={{0,4},{4,8},{8,12},{12,16},{16,20},{20,24},{24,28},{28,0},{1,5},{5... | collective-permute-start | bytes 1032200 | tf_op jit(solution)/shard_map/ppermute | solution.py:18
  249.9 81.7 %collective-permute-start.3 = (bf16[2,2,336,128]{3,1,0,2:T(2,128)(2,1)S(1)}, bf16[2,2,336,128]{3,1,0,2:T(2,128)(2,1)}, u32[]{:S(2)}, u32[]{:S(2)}) collective-permute-start(bf16[2,2,336,128]{3,1,0,2:T(2,128)(2,1)S(1)} %all_gather.14), channel_id=1, source_target_pairs={{4,0},{8,4},{12,8},{16,12},{20,16},{24,20},{28,24},{0,28},{5,1},{9... | collective-permute-start | bytes 1032200 | tf_op jit(solution)/shard_map/ppermute | solution.py:20
  348.3 0.9 copy-start.5
  348.5 107.9 %copy-start.8 = (f32[2,128]{1,0:T(2,128)S(1)}, f32[2,128]{1,0:T(2,128)}, u32[]{:S(2)}) copy-start(f32[2,128]{1,0:T(2,128)} %copy-done.7) | copy-start | bytes 3076
  348.6 107.9 %copy-start.12 = (f32[1,128]{1,0:T(1,128)S(1)}, f32[1,128]{1,0:T(1,128)}, u32[]{:S(2)}) copy-start(f32[1,128]{1,0:T(1,128)} %get-tuple-element.65) | copy-start | bytes 1540
  348.6 107.9 %copy-start.13 = (f32[1,128]{1,0:T(1,128)S(1)}, f32[1,128]{1,0:T(1,128)}, u32[]{:S(2)}) copy-start(f32[1,128]{1,0:T(1,128)} %get-tuple-element.63) | copy-start | bytes 1540
Sparse Core Ops, SparseCore 0:
  67.5 66.7 all-reduce.2
  248.7 75.5 all-reduce.4
